TPU v7x, 32 devices: a whole 2x2x4 slice. The times are simulated.
32 devices in a mesh: ctx: 8 (over y, x, core), tp: 4 (over z).
Axes of the slice: x: 2, y: 2, z: 4, core: 2. Of those that a mesh axis runs over, the one named last changes fastest.
Arguments:
- queries: bfloat16 [2048, 8192], P('ctx', 'tp'), may hold values from -8 to 8
- keys: bfloat16 [2048, 1024], P('ctx'), may hold values from -6 to 6
- values: bfloat16 [2048, 1024], P('ctx'), may hold values from -6 to 6
Outputs:
- attended: bfloat16 [2048, 8192], P('ctx', 'tp')
All inputs are finite; a program needn't handle non-finite values.
Results may differ from a plain program's by a relative error of at most 0.0032.
Values may be sent and summed in bfloat16 or wider, within the bound.
A program may use at most 64 MiB of HBM per device.

v0:
```python
from functools import partial

import jax
import jax.numpy as jnp
from jax import lax
from jax.sharding import PartitionSpec as P

HEADS = 64
KV_HEADS = 8
HEAD_DIM = 128


minimum_score_value = -1e30


def keep_state(hidden_states):
    return hidden_states


def fold_set(hidden_states, query_head_list, query_pos, key_head_list, value_heads, key_pos):
    row_peak, row_total, summed = hidden_states
    score_scale = HEAD_DIM ** (-0.5)
    scores = (
        jnp.einsum(
            "iaxp,vap->axiv", query_head_list, key_head_list, preferred_element_type=jnp.float32
        )
        * score_scale
    )
    allowed = key_pos[None, :] <= query_pos[:, None]
    scores = jnp.where(allowed, scores, minimum_score_value)
    new_peak = jnp.maximum(row_peak, jnp.max(scores, axis=-1))
    raw_weights = jnp.where(allowed, jnp.exp(scores - new_peak[..., None]), 0.0)
    shrink = jnp.exp(row_peak - new_peak)
    row_total = jnp.sum(raw_weights, axis=-1)
    summed = jnp.einsum(
        "cuiz,zca->cuia",
        raw_weights.astype(jnp.bfloat16),
        value_heads,
        preferred_element_type=jnp.float32,
    )
    return (new_peak, row_total, summed)


def attend(query_sets, keys_mine, values_mine, kv_dev, shared):
    shaped = [rows.reshape(rows.shape[0], kv_dev, shared, HEAD_DIM) for rows, _ in query_sets]
    starting = []
    for rows, _ in query_sets:
        row_count = rows.shape[0]
        starting.append(
            (
                jnp.full((kv_dev, shared, row_count), minimum_score_value, jnp.float32),
                jnp.zeros((kv_dev, shared, row_count), jnp.float32),
                jnp.zeros((kv_dev, shared, row_count, HEAD_DIM), jnp.float32),
            )
        )

    def absorb(carried, pieces, start):
        key_piece, value_piece = pieces
        count = key_piece.shape[0]
        key_head_list = key_piece.reshape(count, kv_dev, HEAD_DIM)
        value_heads = value_piece.reshape(count, kv_dev, HEAD_DIM)
        key_pos = jnp.arange(count, dtype=jnp.int32)
        updated = []
        for query_head_list, (_, query_pos), hidden_states in zip(shaped, query_sets, carried):
            worker = partial(
                fold_set,
                query_head_list=query_head_list,
                query_pos=query_pos,
                key_head_list=key_head_list,
                value_heads=value_heads,
                key_pos=key_pos,
            )
            updated.append(lax.cond(start <= query_pos[-1], worker, keep_state, hidden_states))
        return tuple(updated)

    finals = absorb(
        tuple(starting),
        (
            lax.all_gather(keys_mine, "ctx", axis=0, tiled=True),
            lax.all_gather(values_mine, "ctx", axis=0, tiled=True),
        ),
        jnp.int32(0),
    )
    results = []
    for (row_peak, row_total, summed), (rows, _) in zip(finals, query_sets):
        normed = summed / row_total[..., None]
        results.append(
            jnp.transpose(normed, (2, 0, 1, 3))
            .reshape(rows.shape[0], kv_dev * shared * HEAD_DIM)
            .astype(jnp.bfloat16)
        )
    return results


def shards(queries, keys, values):
    context_location = lax.axis_index("ctx")
    tp_place = lax.axis_index("tp")
    tok_dev = queries.shape[0]
    per_dev = queries.shape[1] // HEAD_DIM
    group_size = HEADS // KV_HEADS
    shared = min(group_size, per_dev)
    kv_dev = per_dev // shared
    first_col = tp_place * per_dev // group_size * HEAD_DIM
    keys_mine = lax.dynamic_slice_in_dim(keys, first_col, kv_dev * HEAD_DIM, 1)
    values_mine = lax.dynamic_slice_in_dim(values, first_col, kv_dev * HEAD_DIM, 1)
    half_rows = tok_dev // 2
    row_base = context_location * tok_dev
    offsets = jnp.arange(half_rows, dtype=jnp.int32)
    leading = queries[:half_rows]
    trailing = queries[half_rows:]
    trail_start = row_base + half_rows
    query_sets = ((leading, row_base + offsets), (trailing, trail_start + offsets))
    results = attend(query_sets, keys_mine, values_mine, kv_dev, shared)
    trailing_output = results[1]
    return jnp.concatenate([results[0], trailing_output], 0)


def solution(mesh):
    in_specs = (P("ctx", "tp"), P("ctx", None), P("ctx", None))
    out_specs = P("ctx", "tp")
    return jax.shard_map(shards, mesh=mesh, in_specs=in_specs, out_specs=out_specs, check_vma=False)
```

profile of v0, /device:TPU:5, one launch (start us, length us, event | category | flops | bytes accessed | tf_op | source)
XLA Modules:
  0.0 123.6 jit_solution(17493399732737503379)
XLA Ops:
  6.5 1.0 copy-done
  7.6 0.8 copy.38
  8.4 0.9 constant_dynamic-slice_fusion
  9.4 0.8 copy.39
  10.2 0.6 slice.14
  11.4 0.6 slice.15
  12.7 21.5 %all-gather.3.cloned.1.call-done = bf16[2048,256]{0,1:T(8,128)(2,1)} async-done(((bf16[256,256]{0,1:T(8,128)(2,1)}), bf16[2048,256]{0,1:T(8,128)(2,1)}) %all-gather.3.cloned.1.call-update) | async-done | bytes 1048592 | tf_op jit(solution)/shard_map/all_gather | solution.py:79
  34.2 25.4 %all-gather.5.cloned.1.call-done = bf16[2048,256]{0,1:T(8,128)(2,1)} async-done(((bf16[256,256]{0,1:T(8,128)(2,1)}), bf16[2048,256]{0,1:T(8,128)(2,1)}) %all-gather.5.cloned.1.call-update) | async-done | bytes 1048592 | tf_op jit(solution)/shard_map/all_gather | solution.py:80
  59.6 27.1 %conditional.2 = (f32[2,8,128]{2,1,0:T(8,128)S(1)}, f32[2,8,128,128]{3,2,1,0:T(8,128)S(1)}) conditional(s32[]{:T(128)} %bitcast.8, () %tuple.21, (s32[2048]{0:T(1024)S(1)}, s32[128]{0:T(128)S(1)}, bf16[256,2048]{1,0:T(8,128)(2,1)}, bf16[2048,2,128]{0,2,1:T(8,128)(2,1)}, bf16[2048,2,128]{0,2,1:T(8,128)(2,1)}) %tuple.40), branch_computations={%region_0.1_spmd, %region_1.4_spmd} | conditional | flops 2202269696 | bytes 62448172 | solution.py:73
  59.9 1.5 %copy.14 = bf16[256,2048]{0,1:T(8,128)(2,1)S(1)} copy(bf16[256,2048]{1,0:T(8,128)(2,1)} %get-tuple-element.49) | data formatting | bytes 2097152 | tf_op jit(solution)/shard_map
  61.4 8.3 %fusion = (f32[2,8,128]{2,1,0:T(8,128)S(1)}, f32[2,2048,128,8]{2,1,3,0:T(8,128)}) fusion(pred[128,2048]{0,1:T(8,128)(4,1)S(1)} %broadcast_compare_fusion, bf16[128,2,8,128]{0,3,2,1:T(8,128)(2,1)S(1)} %bitcast.68, bf16[2048,2,128]{0,2,1:T(8,128)(2,1)} %get-tuple-element.50), kind=kOutput, calls=%fused_computation.2 | convolution fusion | flops 1086322688 | bytes 18620416 | tf_op jit(solution)/shard_map/cond/branch_1_fun/iaxp,vap->axiv/dot_general | solution.py:24
  69.8 9.0 %fusion.3 = f32[2,8,128,128]{3,2,1,0:T(8,128)S(1)} fusion(f32[2,2048,128,8]{2,1,3,0:T(8,128)} %get-tuple-element.58, f32[2,8,128]{2,1,0:T(8,128)S(1)} %broadcast_maximum_fusion, pred[128,2048]{0,1:T(8,128)(4,1)S(1)} %broadcast_compare_fusion, bf16[2048,2,128]{0,2,1:T(8,128)(2,1)S(1)} %copy-done.1), kind=kOutput, calls=%fused_computation.5 | convolution fusion | flops 1094713344 | bytes 19144704 | tf_op jit(solution)/shard_map/cond/branch_1_fun/cuiz,zca->cuia/dot_general | solution.py:35
  78.8 7.9 %fusion.2 = f32[2,8,128]{2,1,0:T(8,128)S(1)} fusion(f32[2,2048,128,8]{2,1,3,0:T(8,128)} %get-tuple-element.58, f32[2,8,128]{2,1,0:T(8,128)S(1)} %broadcast_maximum_fusion, pred[128,2048]{0,1:T(8,128)(4,1)S(1)} %broadcast_compare_fusion), kind=kLoop, calls=%fused_computation.4 | loop fusion | flops 20969472 | bytes 17055744 | tf_op jit(solution)/shard_map/cond/branch_1_fun/reduce_sum | solution.py:34
  86.7 0.3 fusion.24
  87.1 0.3 copy.17
  87.4 27.3 %conditional.3 = (f32[2,8,128]{2,1,0:T(8,128)S(1)}, f32[2,8,128,128]{3,2,1,0:T(8,128)S(1)}) conditional(s32[]{:T(128)} %bitcast.12, () %tuple.23, (s32[2048]{0:T(1024)S(1)}, s32[128]{0:T(128)S(1)}, bf16[256,2048]{1,0:T(8,128)(2,1)}, bf16[2048,2,128]{0,2,1:T(8,128)(2,1)}, bf16[2048,2,128]{0,2,1:T(8,128)(2,1)}) %tuple.41), branch_computations={%region_4.5_spmd, %region_5.8_spmd} | conditional | flops 2202269696 | bytes 62448172 | solution.py:73
  87.6 0.3 broadcast_compare_fusion.1
  88.0 1.5 %copy.18 = bf16[256,2048]{0,1:T(8,128)(2,1)S(1)} copy(bf16[256,2048]{1,0:T(8,128)(2,1)} %get-tuple-element.54) | data formatting | bytes 2097152 | tf_op jit(solution)/shard_map
  89.5 8.3 %fusion.12 = (f32[2,8,128]{2,1,0:T(8,128)S(1)}, f32[2,2048,128,8]{2,1,3,0:T(8,128)}) fusion(pred[128,2048]{0,1:T(8,128)(4,1)S(1)} %broadcast_compare_fusion.1, bf16[128,2,8,128]{0,3,2,1:T(8,128)(2,1)S(1)} %bitcast.69, bf16[2048,2,128]{0,2,1:T(8,128)(2,1)} %get-tuple-element.55), kind=kOutput, calls=%fused_computation.17 | convolution fusion | flops 1086322688 | bytes 18620416 | tf_op jit(solution)/shard_map/cond/branch_1_fun/iaxp,vap->axiv/dot_general | solution.py:24
  97.8 9.0 %fusion.15 = f32[2,8,128,128]{3,2,1,0:T(8,128)S(1)} fusion(f32[2,2048,128,8]{2,1,3,0:T(8,128)} %get-tuple-element.60, f32[2,8,128]{2,1,0:T(8,128)S(1)} %broadcast_maximum_fusion.1, pred[128,2048]{0,1:T(8,128)(4,1)S(1)} %broadcast_compare_fusion.1, bf16[2048,2,128]{0,2,1:T(8,128)(2,1)S(1)} %copy-done.2), kind=kOutput, calls=%fused_computation.20 | convolution fusion | flops 1094713344 | bytes 19144704 | tf_op jit(solution)/shard_map/cond/branch_1_fun/cuiz,zca->cuia/dot_general | solution.py:35
  106.9 7.9 %fusion.14 = f32[2,8,128]{2,1,0:T(8,128)S(1)} fusion(f32[2,2048,128,8]{2,1,3,0:T(8,128)} %get-tuple-element.60, f32[2,8,128]{2,1,0:T(8,128)S(1)} %broadcast_maximum_fusion.1, pred[128,2048]{0,1:T(8,128)(4,1)S(1)} %broadcast_compare_fusion.1), kind=kLoop, calls=%fused_computation.19 | loop fusion | flops 20969472 | bytes 17055744 | tf_op jit(solution)/shard_map/cond/branch_1_fun/reduce_sum | solution.py:34
  114.8 0.3 fusion.25
  115.1 0.3 copy.21
  115.7 1.1 pad_maximum_fusion
  (20 shorter events, 0.8 us)
Async XLA Ops:
  6.5 1.0 copy-start
  6.5 27.6 %all-gather.3.cloned.1.call-start = ((), (), s32[]{:S(2)}) async-start(), calls=%async_computation | async-start | bytes 1179648 | tf_op jit(solution)/shard_map/all_gather | solution.py:79
  8.4 51.2 %all-gather.5.cloned.1.call-start = ((), (), s32[]{:S(2)}) async-start(), calls=%async_computation.1 | async-start | bytes 1179648 | tf_op jit(solution)/shard_map/all_gather | solution.py:80
  59.6 10.2 %copy-start.1 = (bf16[2048,2,128]{0,2,1:T(8,128)(2,1)S(1)}, bf16[2048,2,128]{0,2,1:T(8,128)(2,1)}, u32[]{:S(2)}) copy-start(bf16[2048,2,128]{0,2,1:T(8,128)(2,1)} %get-tuple-element.51) | copy-start | bytes 3145732 | tf_op jit(solution)/shard_map/cond
  87.6 10.2 %copy-start.2 = (bf16[2048,2,128]{0,2,1:T(8,128)(2,1)S(1)}, bf16[2048,2,128]{0,2,1:T(8,128)(2,1)}, u32[]{:S(2)}) copy-start(bf16[2048,2,128]{0,2,1:T(8,128)(2,1)} %get-tuple-element.56) | copy-start | bytes 3145732 | tf_op jit(solution)/shard_map/cond
Sparse Core Ops, SparseCore 0:
  9.2 24.9 all-gather.2
  36.0 23.4 all-gather.4
where the time goes:
time: 125 us; the launch traced here: 124 us
  waiting for transfers between devices  46.9 us (38%)
  matrix products  34.7 us (28%)
  other arithmetic  18.2 us (15%)
  between operations  14.8 us (12%)
  local copies, waits for them, and re-layouts  8.69 us (7%)
    all_gather x1, waiting for transfers between devices, attend(): lax.all_gather(values_mine, 'ctx', axis=0, tiled=True)  25.4 us
    all_gather x1, waiting for transfers between devices, attend(): lax.all_gather(keys_mine, 'ctx', axis=0, tiled=True)  21.5 us
    dot_general x2, matrix products, fold_set(): jnp.einsum('cuiz,zca->cuia', raw_weights.astype(jnp.bfloat16), value_head...  18 us
    dot_general x2, matrix products, fold_set(): jnp.einsum('iaxp,vap->axiv', query_head_list, key_head_list, preferred_el...  16.7 us
    reduce_sum x2, other arithmetic, fold_set(): row_total = jnp.sum(raw_weights, axis=-1)  15.8 us
    another operation x2, local copies, waits for them, and re-layouts  2.96 us
    unnamed x4, local copies, waits for them, and re-layouts  2.56 us
  transfers between devices with their start and end apart: 2, of which 2 were waited for; matrix products, arithmetic and copies ran while one was open for 2% of the time, Pallas kernels for 0%

commit v1 on v0

v1 whole, which is shorter than its diff:
```python
import functools
import math

import jax
import jax.numpy as jnp
from jax import lax
from jax.experimental import pallas as pl
from jax.experimental.pallas import tpu as pltpu
from jax.sharding import PartitionSpec as P

HEADS = 64
KV_HEADS = 8
HEAD_DIM = 128
LANES = 128
MASKED = -1e30
EXP2_SCALE = HEAD_DIM ** -0.5 * math.log2(math.e)


def attend_heads(q_v, kv, acc, peak, heads, kv_head, blocks, masked, first):
    cols = pl.ds(pl.multiple_of(kv_head * HEAD_DIM, HEAD_DIM), HEAD_DIM)
    k = jnp.concatenate([kv[b, 0, :, cols] for b in blocks], 0)
    v = jnp.concatenate([kv[b, 1, :, cols] for b in blocks], 0)
    v = jnp.concatenate([v, jnp.ones((v.shape[0], LANES), v.dtype)], 1)
    rows, count = q_v.shape[0], k.shape[0]

    def score(h):
        q = q_v[:, pl.ds(pl.multiple_of(h * HEAD_DIM, HEAD_DIM), HEAD_DIM)]
        return lax.dot_general(q, k, (((1,), (1,)), ((), ())), preferred_element_type=jnp.float32)

    def fold(h, s):
        if masked:
            row = lax.broadcasted_iota(jnp.int32, s.shape, 0)
            col = lax.broadcasted_iota(jnp.int32, s.shape, 1)
            s = jnp.where(col <= row, s, MASKED)
        top = jnp.broadcast_to(jnp.max(s, axis=1, keepdims=True), (rows, LANES))
        if not first:
            before = peak[h]
            top = jnp.maximum(before, top)
        peak[h] = top
        wide = jnp.concatenate([top] * (count // LANES), 1)
        w = jnp.exp2((s - wide) * EXP2_SCALE).astype(jnp.bfloat16)
        new = jnp.dot(w, v, preferred_element_type=jnp.float32)
        if not first:
            shrink = jnp.exp2((before - top) * EXP2_SCALE)
            new = acc[h] * jnp.concatenate([shrink, shrink], 1) + new
        acc[h] = new

    ready = score(heads[0])
    for i, h in enumerate(heads):
        upcoming = score(heads[i + 1]) if i + 1 < len(heads) else None
        fold(h, ready)
        ready = upcoming


def kernel(nc, per_dev, group, kv_dev, q_hbm, k_hbm, v_hbm, o_ref,
           q_v, kv, acc, peak, loc_sem, send_sem, fwd_sem, recv_sem):
    c = lax.axis_index("ctx")
    tp = lax.axis_index("tp")
    odd = lax.rem(c, 2)
    partner = c + 1 - 2 * odd
    shared = per_dev // kv_dev
    chunk = min(4, shared)
    first_col = pl.multiple_of(tp * per_dev // group * HEAD_DIM, HEAD_DIM)
    src = pl.ds(first_col, kv_dev * HEAD_DIM)
    load_k = pltpu.make_async_copy(k_hbm.at[:, src], kv.at[c, 0], loc_sem.at[0])
    load_v = pltpu.make_async_copy(v_hbm.at[:, src], kv.at[c, 1], loc_sem.at[1])
    load_q = pltpu.make_async_copy(q_hbm, q_v, loc_sem.at[2])
    load_k.start()
    load_v.start()
    load_q.start()

    barrier = pltpu.get_barrier_semaphore()
    pl.semaphore_signal(barrier, inc=1, device_id={"ctx": partner})
    for i in range(1, nc // 2):
        pl.semaphore_signal(barrier, inc=1, device_id={"ctx": lax.rem(c + 2 * i, nc)})
    pl.semaphore_wait(barrier, nc // 2)

    def copy_to(b, target, sem):
        return pltpu.make_async_remote_copy(
            src_ref=kv.at[b], dst_ref=kv.at[b], send_sem=sem, recv_sem=recv_sem.at[b],
            device_id={"ctx": target})

    load_k.wait()
    load_v.wait()
    sends = [(odd == 0, copy_to(c, partner, send_sem.at[0]))]
    for i in range(1, nc // 2):
        sends.append((c + 2 * i < nc, copy_to(c, lax.rem(c + 2 * i, nc), send_sem.at[i])))
    for wanted, copy in sends:
        pl.when(wanted)(copy.start)
    load_q.wait()

    def forward(p):
        mine = 2 * p + odd
        copy = copy_to(mine, partner, fwd_sem.at[p])
        copy.wait_recv()
        copy.start()

    def sweep(blocks, masked, first):
        def body(n, carry):
            heads = [n * chunk + i for i in range(chunk)]
            attend_heads(q_v, kv, acc, peak, heads, n * chunk // shared, blocks, masked, first)
            return carry
        return body

    chunks = per_dev // chunk
    pairs = c // 2
    lax.fori_loop(0, chunks, sweep([c], True, True), 0)

    @pl.when(odd == 1)
    def _():
        copy_to(c - 1, partner, send_sem.at[0]).wait_recv()
        lax.fori_loop(0, chunks, sweep([c - 1], False, False), 0)

    @pl.when(pairs > 0)
    def _():
        forward(pairs - 1)

    def pair_step(t, carry):
        p = pairs - 1 - t
        copy_to(2 * p + 1 - odd, partner, fwd_sem.at[p]).wait_recv()
        body = sweep([2 * p, 2 * p + 1], False, False)
        half = chunks // 2
        lax.fori_loop(0, half, body, 0)

        @pl.when(p > 0)
        def _():
            forward(p - 1)

        lax.fori_loop(half, chunks, body, 0)
        return carry

    lax.fori_loop(0, pairs, pair_step, 0)

    def finish(h, carry):
        out = acc[h, :, :LANES] / acc[h, :, LANES:]
        o_ref[:, pl.ds(pl.multiple_of(h * HEAD_DIM, HEAD_DIM), HEAD_DIM)] = out.astype(o_ref.dtype)
        return carry

    lax.fori_loop(0, per_dev, finish, 0)

    def drain(p, carry):
        copy_to(2 * p + odd, partner, fwd_sem.at[p]).wait_send()
        return carry

    lax.fori_loop(0, pairs, drain, 0)
    for wanted, copy in sends:
        pl.when(wanted)(copy.wait_send)


def solution(mesh):
    nc = mesh.shape["ctx"]

    def step(queries, keys, values):
        rows, width = queries.shape
        per_dev = width // HEAD_DIM
        group = HEADS // KV_HEADS
        kv_dev = per_dev // min(group, per_dev)
        any_space = pl.BlockSpec(memory_space=pltpu.HBM)
        return pl.pallas_call(
            functools.partial(kernel, nc, per_dev, group, kv_dev),
            out_shape=jax.ShapeDtypeStruct((rows, width), jnp.bfloat16),
            in_specs=[any_space] * 3,
            out_specs=pl.BlockSpec(memory_space=pltpu.VMEM),
            scratch_shapes=[
                pltpu.VMEM((rows, width), jnp.bfloat16),
                pltpu.VMEM((nc, 2, rows, kv_dev * HEAD_DIM), jnp.bfloat16),
                pltpu.VMEM((per_dev, rows, 2 * LANES), jnp.float32),
                pltpu.VMEM((per_dev, rows, LANES), jnp.float32),
                pltpu.SemaphoreType.DMA((3,)),
                pltpu.SemaphoreType.DMA((max(nc // 2, 1),)),
                pltpu.SemaphoreType.DMA((max(nc // 2, 1),)),
                pltpu.SemaphoreType.DMA((nc,)),
            ],
            compiler_params=pltpu.CompilerParams(
                collective_id=0, has_side_effects=True, vmem_limit_bytes=48 * 1024 * 1024),
        )(queries, keys, values)

    return jax.shard_map(
        step, mesh=mesh,
        in_specs=(P("ctx", "tp"), P("ctx", None), P("ctx", None)),
        out_specs=P("ctx", "tp"), check_vma=False)
```

time: 125 us -> 26.5 us (0.21)
  the two profiles are of different devices: /device:TPU:5 before, /device:TPU:7 now
where the time goes in v1:
time: 26.5 us; the launch traced here: 26.3 us
  Pallas kernels  22 us (83%)
  local copies, waits for them, and re-layouts  4.28 us (16%)
    pallas_call x1, Pallas kernels, step(): pl.pallas_call(functools.partial(kernel, nc, per_dev, group, kv_dev), out...  22 us
    unnamed x7, local copies, waits for them, and re-layouts  4.28 us

profile of v1, /device:TPU:7, one launch (start us, length us, event | category | flops | bytes accessed | tf_op | source)
XLA Modules:
  0.0 26.3 jit_solution(16207570674505771703)
XLA Ops:
  0.0 0.0 copy-start
  0.0 1.2 %copy-done = bf16[256,2048]{1,0:T(8,128)(2,1)S(1)} copy-done((bf16[256,2048]{1,0:T(8,128)(2,1)S(1)}, bf16[256,2048]{1,0:T(8,128)(2,1)}, u32[]{:S(2)}) %copy-start) | copy-done | bytes 1048600
  1.2 0.0 copy-start.1
  1.2 1.0 %copy-done.1 = bf16[256,1024]{1,0:T(8,128)(2,1)S(1)} copy-done((bf16[256,1024]{1,0:T(8,128)(2,1)S(1)}, bf16[256,1024]{1,0:T(8,128)(2,1)}, u32[]{:S(2)}) %copy-start.1) | copy-done | bytes 524312
  2.3 0.0 copy-start.2
  2.3 1.0 %copy-done.2 = bf16[256,1024]{1,0:T(8,128)(2,1)S(1)} copy-done((bf16[256,1024]{1,0:T(8,128)(2,1)S(1)}, bf16[256,1024]{1,0:T(8,128)(2,1)}, u32[]{:S(2)}) %copy-start.2) | copy-done | bytes 524312
  3.3 22.0 %shard_map.37 = bf16[256,2048]{1,0:T(8,128)(2,1)S(1)} custom-call(bf16[256,2048]{1,0:T(8,128)(2,1)S(1)} %copy-done, bf16[256,1024]{1,0:T(8,128)(2,1)S(1)} %copy-done.1, bf16[256,1024]{1,0:T(8,128)(2,1)S(1)} %copy-done.2), custom_call_target="tpu_custom_call" | custom-call | tf_op jit(solution)/shard_map/pallas_call | solution.py:159
  25.3 1.0 %copy.5 = bf16[256,2048]{1,0:T(8,128)(2,1)} copy(bf16[256,2048]{1,0:T(8,128)(2,1)S(1)} %shard_map.37) | data formatting | bytes 2097152
Async XLA Ops:
  0.0 1.2 %copy-start = (bf16[256,2048]{1,0:T(8,128)(2,1)S(1)}, bf16[256,2048]{1,0:T(8,128)(2,1)}, u32[]{:S(2)}) copy-start(bf16[256,2048]{1,0:T(8,128)(2,1)} %q_hbm.1) | copy-start | bytes 3145732
  1.2 1.0 %copy-start.1 = (bf16[256,1024]{1,0:T(8,128)(2,1)S(1)}, bf16[256,1024]{1,0:T(8,128)(2,1)}, u32[]{:S(2)}) copy-start(bf16[256,1024]{1,0:T(8,128)(2,1)} %k_hbm.1) | copy-start | bytes 1572868
  2.3 1.0 %copy-start.2 = (bf16[256,1024]{1,0:T(8,128)(2,1)S(1)}, bf16[256,1024]{1,0:T(8,128)(2,1)}, u32[]{:S(2)}) copy-start(bf16[256,1024]{1,0:T(8,128)(2,1)} %v_hbm.1) | copy-start | bytes 1572868

commit v2 on v1

v2 whole, which is shorter than its diff:
```python
import functools
import math

import jax
import jax.numpy as jnp
from jax import lax
from jax.experimental import pallas as pl
from jax.experimental.pallas import tpu as pltpu
from jax.sharding import PartitionSpec as P

HEADS = 64
KV_HEADS = 8
HEAD_DIM = 128
LANES = 128
MASKED = -1e30
EXP2_SCALE = HEAD_DIM ** -0.5 * math.log2(math.e)


def attend_heads(q_v, kv, acc, peak, heads, kv_head, blocks, masked, first):
    k = jnp.concatenate([kv[b, kv_head, 0] for b in blocks], 0)
    v = jnp.concatenate([kv[b, kv_head, 1] for b in blocks], 0)
    v = jnp.concatenate([v, jnp.ones((v.shape[0], LANES), v.dtype)], 1)
    rows, count = q_v.shape[0], k.shape[0]

    def score(h):
        q = q_v[:, pl.ds(pl.multiple_of(h * HEAD_DIM, HEAD_DIM), HEAD_DIM)]
        return lax.dot_general(q, k, (((1,), (1,)), ((), ())), preferred_element_type=jnp.float32)

    def fold(h, s):
        if masked:
            row = lax.broadcasted_iota(jnp.int32, s.shape, 0)
            col = lax.broadcasted_iota(jnp.int32, s.shape, 1)
            s = jnp.where(col <= row, s, MASKED)
        top = jnp.broadcast_to(jnp.max(s, axis=1, keepdims=True), (rows, LANES))
        if not first:
            before = peak[h]
            top = jnp.maximum(before, top)
        peak[h] = top
        wide = jnp.concatenate([top] * (count // LANES), 1)
        w = jnp.exp2((s - wide) * EXP2_SCALE).astype(jnp.bfloat16)
        new = jnp.dot(w, v, preferred_element_type=jnp.float32)
        if not first:
            shrink = jnp.exp2((before - top) * EXP2_SCALE)
            new = acc[h] * jnp.concatenate([shrink, shrink], 1) + new
        acc[h] = new

    ready = score(heads[0])
    for i, h in enumerate(heads):
        upcoming = score(heads[i + 1]) if i + 1 < len(heads) else None
        fold(h, ready)
        ready = upcoming


def kernel(nc, per_dev, group, kv_dev, q_hbm, k_hbm, v_hbm, o_ref,
           q_v, kv, acc, peak, loc_sem, send_sem, fwd_sem, far_sem, recv_sem):
    c = lax.axis_index("ctx")
    tp = lax.axis_index("tp")
    odd = lax.rem(c, 2)
    pair = c // 2
    partner = c + 1 - 2 * odd
    shared = per_dev // kv_dev
    chunk = min(4, shared)
    square = nc == 8 and kv_dev == 2
    base = tp * per_dev // group

    loads = []
    for g in range(kv_dev):
        cols = pl.ds(pl.multiple_of((base + g) * HEAD_DIM, HEAD_DIM), HEAD_DIM)
        loads.append([
            pltpu.make_async_copy(ref.at[:, cols], kv.at[c, g, i], loc_sem.at[2 * g + i])
            for i, ref in enumerate((k_hbm, v_hbm))])
        for load in loads[g]:
            load.start()
    load_q = pltpu.make_async_copy(q_hbm, q_v, loc_sem.at[2 * kv_dev])
    load_q.start()

    barrier = pltpu.get_barrier_semaphore()
    pl.semaphore_signal(barrier, inc=1, device_id={"ctx": partner})
    for i in range(1, nc // 2):
        pl.semaphore_signal(barrier, inc=1, device_id={"ctx": lax.rem(c + 2 * i, nc)})
    pl.semaphore_wait(barrier, nc // 2)

    def copy_to(b, g, target, sem):
        return pltpu.make_async_remote_copy(
            src_ref=kv.at[b, g], dst_ref=kv.at[b, g], send_sem=sem, recv_sem=recv_sem.at[b, g],
            device_id={"ctx": target})

    for load in sum(loads, []):
        load.wait()
    sends = []
    for g in range(kv_dev):
        sends.append((odd == 0, copy_to(c, g, partner, send_sem.at[0, g])))
        if square:
            sends.append((lax.rem(pair, 2) == 0, copy_to(c, g, lax.rem(c + 2, nc), send_sem.at[1, g])))
            first = kv_dev - 1 - g
            other = lax.select(pair == 0, first, g)
            sends.append((pair < 2, copy_to(c, other, lax.rem(c + 4, nc), send_sem.at[2, g])))
        else:
            for i in range(1, nc // 2):
                sends.append((c + 2 * i < nc, copy_to(c, g, lax.rem(c + 2 * i, nc), send_sem.at[i, g])))
    for wanted, copy in sends:
        pl.when(wanted)(copy.start)
    load_q.wait()

    def item(t):
        if not square:
            return pair - 1 - t // kv_dev, lax.rem(t, kv_dev)
        third = (lax.select(t < 4, 2 - lax.rem(t, 2), 0), lax.select(t < 4, t // 2, t - 4))
        second = (t // 2, lax.rem((t + 1) // 2 + 1, 2))
        return (lax.select(pair == 3, third[0], lax.select(pair == 2, second[0], 0)),
                lax.select(pair == 3, third[1], lax.select(pair == 2, second[1], t)))

    def onward(p, g):
        mine = 2 * p + odd
        up = ((pair == 1) & (g == 0)) | ((pair == 2) & (p == 0) & (g == 1))
        back = (pair == 3) & (p == 1)
        target = lax.select(pair == 3, 4 + odd, 6 + odd)
        return up | back, copy_to(mine, g, target, far_sem.at[p, g])

    def pull(t):
        p, g = item(t)
        copy = copy_to(2 * p + odd, g, partner, fwd_sem.at[p, g])
        copy.wait_recv()
        if square:
            wanted, far = onward(p, g)
            pl.when(wanted)(far.start)
        copy.start()

    def sweep(blocks, kv_head, masked, first):
        def body(n, carry):
            heads = [n * chunk + i for i in range(chunk)]
            g = n * chunk // shared if kv_head is None else kv_head
            attend_heads(q_v, kv, acc, peak, heads, g, blocks, masked, first)
            return carry
        return body

    def finish(h, carry):
        out = acc[h, :, :LANES] / acc[h, :, LANES:]
        o_ref[:, pl.ds(pl.multiple_of(h * HEAD_DIM, HEAD_DIM), HEAD_DIM)] = out.astype(o_ref.dtype)
        return carry

    chunks = per_dev // chunk
    steps = pair * kv_dev
    lax.fori_loop(0, chunks, sweep([c], None, True, True), 0)

    @pl.when(odd == 1)
    def _():
        for g in range(kv_dev):
            copy_to(c - 1, g, partner, send_sem.at[0, g]).wait_recv()
        lax.fori_loop(0, chunks, sweep([c - 1], None, False, False), 0)

    @pl.when(pair > 0)
    def _():
        pull(0)

    def step(t, carry):
        p, g = item(t)
        copy_to(2 * p + 1 - odd, g, partner, fwd_sem.at[p, g]).wait_recv()
        body = sweep([2 * p, 2 * p + 1], g, False, False)
        per_head = shared // chunk
        start = g * per_head
        half = start + per_head // 2
        lax.fori_loop(start, half, body, 0)

        @pl.when(t + 1 < steps)
        def _():
            pull(t + 1)

        lax.fori_loop(half, start + per_head, body, 0)

        @pl.when(t >= steps - kv_dev)
        def _():
            lax.fori_loop(g * shared, (g + 1) * shared, finish, 0)
        return carry

    lax.fori_loop(0, steps, step, 0)

    @pl.when(pair == 0)
    def _():
        lax.fori_loop(0, per_dev, finish, 0)

    def drain(t, carry):
        p, g = item(t)
        copy_to(2 * p + odd, g, partner, fwd_sem.at[p, g]).wait_send()
        if square:
            wanted, far = onward(p, g)
            pl.when(wanted)(far.wait_send)
        return carry

    lax.fori_loop(0, steps, drain, 0)
    for wanted, copy in sends:
        pl.when(wanted)(copy.wait_send)


def solution(mesh):
    nc = mesh.shape["ctx"]

    def step(queries, keys, values):
        rows, width = queries.shape
        per_dev = width // HEAD_DIM
        group = HEADS // KV_HEADS
        kv_dev = per_dev // min(group, per_dev)
        any_space = pl.BlockSpec(memory_space=pltpu.HBM)
        return pl.pallas_call(
            functools.partial(kernel, nc, per_dev, group, kv_dev),
            out_shape=jax.ShapeDtypeStruct((rows, width), jnp.bfloat16),
            in_specs=[any_space] * 3,
            out_specs=pl.BlockSpec(memory_space=pltpu.VMEM),
            scratch_shapes=[
                pltpu.VMEM((rows, width), jnp.bfloat16),
                pltpu.VMEM((nc, kv_dev, 2, rows, HEAD_DIM), jnp.bfloat16),
                pltpu.VMEM((per_dev, rows, 2 * LANES), jnp.float32),
                pltpu.VMEM((per_dev, rows, LANES), jnp.float32),
                pltpu.SemaphoreType.DMA((2 * kv_dev + 1,)),
                pltpu.SemaphoreType.DMA((nc // 2, kv_dev)),
                pltpu.SemaphoreType.DMA((nc // 2, kv_dev)),
                pltpu.SemaphoreType.DMA((nc // 2, kv_dev)),
                pltpu.SemaphoreType.DMA((nc, kv_dev)),
            ],
            compiler_params=pltpu.CompilerParams(
                collective_id=0, has_side_effects=True, vmem_limit_bytes=60 * 1024 * 1024),
        )(queries, keys, values)

    return jax.shard_map(
        step, mesh=mesh,
        in_specs=(P("ctx", "tp"), P("ctx", None), P("ctx", None)),
        out_specs=P("ctx", "tp"), check_vma=False)
```

time: 26.5 us -> 25.7 us (0.970)
  the two profiles are of different devices: /device:TPU:7 before, /device:TPU:5 now
where the time goes in v2:
time: 25.7 us; the launch traced here: 25.5 us
  Pallas kernels  23.2 us (90%)
  local copies, waits for them, and re-layouts  2.3 us (9%)
    pallas_call x1, Pallas kernels, step(): pl.pallas_call(functools.partial(kernel, nc, per_dev, group, kv_dev), out...  23.2 us
    unnamed x1, local copies, waits for them, and re-layouts  2.3 us

profile of v2, /device:TPU:5, one launch (start us, length us, event | category | flops | bytes accessed | tf_op | source)
XLA Modules:
  0.0 25.5 jit_solution(18430066823736322229)
XLA Ops:
  0.0 23.2 %shard_map.37 = bf16[256,2048]{1,0:T(8,128)(2,1)} custom-call(bf16[256,2048]{1,0:T(8,128)(2,1)} %q_hbm.1, bf16[256,1024]{1,0:T(8,128)(2,1)} %k_hbm.1, bf16[256,1024]{1,0:T(8,128)(2,1)} %v_hbm.1), custom_call_target="tpu_custom_call" | custom-call | tf_op jit(solution)/shard_map/pallas_call | solution.py:204
  23.2 2.3 %copy.5 = bf16[256,2048]{1,0:T(8,128)(2,1)} copy(bf16[256,2048]{1,0:T(8,128)(2,1)} %shard_map.37) | data formatting | bytes 2097152

commit v3 on v2

--- a/solution.py
+++ b/solution.py
@@ -13,6 +13,9 @@
 HEAD_DIM = 128
 LANES = 128
 MASKED = -1e30
+CHUNK = 8
+DEPTH = 1
+ROUTED = 1
 EXP2_SCALE = HEAD_DIM ** -0.5 * math.log2(math.e)
 
 
@@ -44,11 +47,11 @@
             new = acc[h] * jnp.concatenate([shrink, shrink], 1) + new
         acc[h] = new
 
-    ready = score(heads[0])
+    ahead = [score(h) for h in heads[:DEPTH]]
     for i, h in enumerate(heads):
-        upcoming = score(heads[i + 1]) if i + 1 < len(heads) else None
-        fold(h, ready)
-        ready = upcoming
+        if i + DEPTH < len(heads):
+            ahead.append(score(heads[i + DEPTH]))
+        fold(h, ahead.pop(0))
 
 
 def kernel(nc, per_dev, group, kv_dev, q_hbm, k_hbm, v_hbm, o_ref,
@@ -59,7 +62,7 @@
     pair = c // 2
     partner = c + 1 - 2 * odd
     shared = per_dev // kv_dev
-    chunk = min(4, shared)
+    chunk = min(CHUNK, shared)
     square = nc == 8 and kv_dev == 2
     base = tp * per_dev // group
 
@@ -91,7 +94,8 @@
     for g in range(kv_dev):
         sends.append((odd == 0, copy_to(c, g, partner, send_sem.at[0, g])))
         if square:
-            sends.append((lax.rem(pair, 2) == 0, copy_to(c, g, lax.rem(c + 2, nc), send_sem.at[1, g])))
+            beside = (lax.rem(pair, 2) == 0) if g < ROUTED else (pair < 3)
+            sends.append((beside, copy_to(c, g, lax.rem(c + 2, nc), send_sem.at[1, g])))
             first = kv_dev - 1 - g
             other = lax.select(pair == 0, first, g)
             sends.append((pair < 2, copy_to(c, other, lax.rem(c + 4, nc), send_sem.at[2, g])))
@@ -113,7 +117,7 @@
     def onward(p, g):
         mine = 2 * p + odd
         up = ((pair == 1) & (g == 0)) | ((pair == 2) & (p == 0) & (g == 1))
-        back = (pair == 3) & (p == 1)
+        back = (pair == 3) & (p == 1) & (g < ROUTED)
         target = lax.select(pair == 3, 4 + odd, 6 + odd)
         return up | back, copy_to(mine, g, target, far_sem.at[p, g])
 
@@ -157,16 +161,13 @@
         p, g = item(t)
         copy_to(2 * p + 1 - odd, g, partner, fwd_sem.at[p, g]).wait_recv()
         body = sweep([2 * p, 2 * p + 1], g, False, False)
-        per_head = shared // chunk
-        start = g * per_head
-        half = start + per_head // 2
-        lax.fori_loop(start, half, body, 0)
 
         @pl.when(t + 1 < steps)
         def _():
             pull(t + 1)
 
-        lax.fori_loop(half, start + per_head, body, 0)
+        per_head = shared // chunk
+        lax.fori_loop(g * per_head, (g + 1) * per_head, body, 0)
 
         @pl.when(t >= steps - kv_dev)
         def _():
@@ -203,7 +204,7 @@
         any_space = pl.BlockSpec(memory_space=pltpu.HBM)
         return pl.pallas_call(
             functools.partial(kernel, nc, per_dev, group, kv_dev),
-            out_shape=jax.ShapeDtypeStruct((rows, width), jnp.bfloat16),
+            out_shape=pltpu.VMEM((rows, width), jnp.bfloat16),
             in_specs=[any_space] * 3,
             out_specs=pl.BlockSpec(memory_space=pltpu.VMEM),
             scratch_shapes=[

time: 25.7 us -> 20.6 us (0.80)
  Pallas kernels: 23.2 us -> 19.5 us
  local copies, waits for them, and re-layouts: 2.3 us -> 0.97 us
    pallas_call x1, Pallas kernels: 23.2 us -> 19.5 us  [step(): pl.pallas_call(functools.partial(kernel, nc, per_dev, group, kv_dev), out...]
    unnamed x1, local copies, waits for them, and re-layouts: 2.3 us -> 0.97 us
where the time goes in v3:
time: 20.6 us; the launch traced here: 20.5 us
  Pallas kernels  19.5 us (95%)
  local copies, waits for them, and re-layouts  0.97 us (5%)
    pallas_call x1, Pallas kernels, step(): pl.pallas_call(functools.partial(kernel, nc, per_dev, group, kv_dev), out...  19.5 us
    unnamed x1, local copies, waits for them, and re-layouts  0.97 us

profile of v3, /device:TPU:5, one launch (start us, length us, event | category | flops | bytes accessed | tf_op | source)
XLA Modules:
  0.0 20.5 jit_solution(8574051706928107752)
XLA Ops:
  0.0 19.5 %shard_map.37 = bf16[256,2048]{1,0:T(8,128)(2,1)S(1)} custom-call(bf16[256,2048]{1,0:T(8,128)(2,1)} %q_hbm.1, bf16[256,1024]{1,0:T(8,128)(2,1)} %k_hbm.1, bf16[256,1024]{1,0:T(8,128)(2,1)} %v_hbm.1), custom_call_target="tpu_custom_call" | custom-call | tf_op jit(solution)/shard_map/pallas_call | solution.py:205
  19.5 1.0 %copy.5 = bf16[256,2048]{1,0:T(8,128)(2,1)} copy(bf16[256,2048]{1,0:T(8,128)(2,1)S(1)} %shard_map.37) | data formatting | bytes 2097152
